TPU v7x, 128 devices: a whole 4x4x4 slice. The times are simulated.
128 devices in a mesh: lat: 4 (over x_hi, core), lon: 4 (over z), lev: 8 (over y, x_lo).
Axes of the slice: x: 4 (x_hi: 2, x_lo: 2; x = x_hi * 2 + x_lo), y: 4, z: 4, core: 2. Of those that a mesh axis runs over, the one named last changes fastest.
Arguments:
- initial_heat: float32 [128, 512, 32, 128], P('lat', 'lon', 'lev'), may hold values from 0.5 to 2
- diffusivity_ratio: float32 [128, 512, 32, 128], P('lat', 'lon', 'lev'), may hold values from 0.03 to 0.15
- forcing_term: float32 [128, 512, 32, 128], P('lat', 'lon', 'lev'), may hold values from -0.2 to 0.2
Outputs:
- standard_deviation_score: float32 [128, 512, 32, 128], P('lat', 'lon', 'lev')
- temperature_end: float32 [128, 512, 32, 128], P('lat', 'lon', 'lev')
All inputs are finite; a program needn't handle non-finite values.
Results may differ from a plain program's by a relative error of at most 0.00002.
Values sent between devices are 32-bit elements; how exact they have to be, the bound alone decides.
A program may use at most 128 MiB of HBM per device.

v0:
```python
import jax
import jax.numpy as jnp
from jax import lax
from jax.sharding import PartitionSpec as P

STEPS = 4


def padded(x, sides, width):
    edges = {}
    for axis, dim in sides:
        size, length = (lax.axis_size(axis), x.shape[dim])
        up = [(i, (i + 1) % size) for i in range(size)]
        last = lax.slice_in_dim(x, length - width, length, axis=dim)
        first = lax.slice_in_dim(x, 0, width, axis=dim)
        edges[dim] = (
            lax.ppermute(last, axis, up),
            lax.ppermute(first, axis, [(b, a) for a, b in up]),
        )
    done = []
    for _, dim in sides:
        low, high = edges[dim]
        around = [(width, width) if d in done else (0, 0) for d in range(x.ndim)]
        x = jnp.concatenate([jnp.pad(low, around), x, jnp.pad(high, around)], axis=dim)
        done.append(dim)
    return x


def sent_to_all(x, axis):
    copies = jnp.broadcast_to(x, (lax.axis_size(axis), *x.shape))
    return lax.all_to_all(copies, axis, split_axis=0, concat_axis=0, tiled=True)


def taken_together(x, axis):
    everything = sent_to_all(x, axis)
    return jnp.sum(everything, axis=0)


def packed_total(arrays, axis):
    ends = [0]
    for a in arrays:
        ends.append(ends[-1] + a.size)
    so_far = taken_together(jnp.concatenate([a.ravel() for a in arrays]), axis)
    return tuple((so_far[b:e].reshape(a.shape) for a, b, e in zip(arrays, ends, ends[1:])))


def without_rim(values, dims):
    for dim in dims:
        values = lax.slice_in_dim(values, 1, values.shape[dim] - 1, axis=dim)
    return values


def shifted_cells(values, dim, start, dims):
    others = [other for other in dims if other != dim]
    values = without_rim(values, others)
    return lax.slice_in_dim(values, start, start + values.shape[dim] - 2, axis=dim)


def march_forward(extended_grid_state, diffusivity_ratio, forcing_term):
    middle = without_rim(extended_grid_state, (0, 1, 2))
    lower = [shifted_cells(extended_grid_state, dim, 0, (0, 1, 2)) for dim in (0, 1, 2)]
    upper = [shifted_cells(extended_grid_state, dim, 2, (0, 1, 2)) for dim in (0, 1, 2)]
    spread = lower[0] + upper[0] + lower[1] + upper[1] + lower[2] + upper[2] - 6.0 * middle
    return middle + diffusivity_ratio * spread + forcing_term


def local(initial_heat, diffusivity_ratio, forcing_term):
    for step in range(STEPS):
        extended_grid_state = padded(initial_heat, (("lat", 0), ("lon", 1), ("lev", 2)), 1)
        initial_heat = march_forward(extended_grid_state, diffusivity_ratio, forcing_term)
    number_of_entries = initial_heat.shape[1] * lax.axis_size("lon")
    guess = 1.0
    moved = initial_heat - guess
    totals, squares = packed_total(
        (jnp.sum(moved, axis=1, keepdims=True), jnp.sum(moved * moved, axis=1, keepdims=True)),
        "lon",
    )
    row_mean_estimate = guess + totals / number_of_entries
    deviations_from_mean = initial_heat - row_mean_estimate
    line_variance = squares / number_of_entries - totals / number_of_entries * (
        totals / number_of_entries
    )
    standard_deviation_score = deviations_from_mean * lax.rsqrt(line_variance + 0.0001)
    return (standard_deviation_score, initial_heat)


def solution(mesh):
    placed = (
        P("lat", "lon", "lev", None),
        P("lat", "lon", "lev", None),
        P("lat", "lon", "lev", None),
    )
    return jax.shard_map(
        local,
        mesh=mesh,
        in_specs=placed,
        out_specs=(P("lat", "lon", "lev", None), P("lat", "lon", "lev", None)),
        check_vma=False,
    )
```

profile of v0, /device:TPU:0, one launch (start us, length us, event | category | flops | bytes accessed | tf_op | source)
XLA Modules:
  0.0 595.5 jit_solution(13675427221701031850)
XLA Ops:
  0.6 4.7 copy.58
  5.3 0.0 copy-start
  5.3 0.5 fusion.58
  5.8 1.7 collective-permute-start.4
  7.5 2.5 collective-permute-start.5
  10.0 0.1 collective-permute-start
  10.1 0.1 fusion.59
  10.2 2.1 collective-permute-start.2
  12.3 2.2 collective-permute-start.3
  14.5 2.2 collective-permute-done.2
  16.7 3.4 collective-permute-start.1
  20.2 84.8 %collective-permute-done = f32[1,128,4,128]{3,1,2,0:T(8,128)S(1)} collective-permute-done((f32[1,128,4,128]{3,1,2,0:T(8,128)S(1)}, f32[1,128,4,128]{3,1,2,0:T(8,128)S(1)}, u32[]{:S(2)}, u32[]{:S(2)}) %collective-permute-start) | collective-permute-done | bytes 262176 | tf_op jit(solution)/shard_map/ppermute | solution.py:17
  105.0 0.7 constant_dynamic-update-slice_fusion.2
  105.7 8.4 %constant_dynamic-update-slice_fusion.1 = f32[34,128,4,128]{3,1,2,0:T(8,128)} fusion(f32[34,128,4,128]{3,1,2,0:T(8,128)} %constant_dynamic-update-slice_fusion.2, f32[32,128,4,128]{3,2,1,0:T(4,128)} %param.3), kind=kLoop, calls=%fused_computation.121 | loop fusion | bytes 16777216
  114.1 0.0 collective-permute-done.1
  114.1 0.7 constant_dynamic-update-slice_fusion
  114.9 30.7 %fusion.38 = f32[32,128,4,128]{3,1,2,0:T(8,128)} fusion(f32[32,128,4,128]{3,1,2,0:T(8,128)} %copy-done, f32[32,128,1,128]{3,1,2,0:T(8,128)} %collective-permute-done.5, f32[34,1,4,128]{3,1,2,0:T(1,128)S(1)} %pad.51, f32[34,128,4,128]{3,1,2,0:T(8,128)} %constant_dynamic-update-slice_fusion, f32[34,1,4,128]{3,1,2,0:T(1,128)S(1)} %pad.50, ...), kind=kLoop, calls=%fused_computation.93 | loop fusion | flops 54525952 | bytes 47325184 | tf_op jit(solution)/shard_map/add | solution.py:64
  145.6 2.5 fusion.55
  148.1 1.3 collective-permute-start.10
  149.4 2.9 collective-permute-start.11
  152.3 1.1 fusion.56
  153.4 0.1 collective-permute-start.6
  153.5 3.2 collective-permute-start.7
  156.7 1.3 fusion.57
  158.0 2.0 collective-permute-start.8
  160.0 4.4 collective-permute-done.8
  164.4 2.2 collective-permute-start.9
  166.7 2.2 collective-permute-done.9
  168.9 74.4 %collective-permute-done.6 = f32[1,128,4,128]{3,1,2,0:T(8,128)S(1)} collective-permute-done((f32[1,128,4,128]{3,1,2,0:T(8,128)S(1)}, f32[1,128,4,128]{3,1,2,0:T(8,128)S(1)}, u32[]{:S(2)}, u32[]{:S(2)}) %collective-permute-start.6) | collective-permute-done | bytes 262176 | tf_op jit(solution)/shard_map/ppermute | solution.py:17
  243.3 1.3 copy-done.1
  244.7 33.3 %fusion.27 = f32[32,128,4,128]{3,1,2,0:T(8,128)} fusion(f32[32,128,4,128]{3,1,2,0:T(8,128)} %fusion.38, f32[32,128,1,128]{3,1,2,0:T(8,128)} %collective-permute-done.11, f32[34,1,4,128]{3,1,2,0:T(1,128)S(1)} %pad.55, f32[34,1,4,128]{3,1,2,0:T(1,128)S(1)} %pad.54, f32[1,128,4,128]{3,1,2,0:T(8,128)S(1)} %collective-permute-done.7, ...), kind=kLoop, calls=%fused_computation.64 | loop fusion | flops 71303168 | bytes 38412288 | tf_op jit(solution)/shard_map/add | solution.py:64
  278.0 2.5 fusion.52
  280.5 1.0 collective-permute-start.16
  281.5 3.2 collective-permute-start.17
  284.7 1.1 fusion.53
  285.8 1.8 collective-permute-start.12
  287.6 1.6 collective-permute-start.13
  289.1 1.3 fusion.54
  290.4 2.0 collective-permute-start.14
  292.4 4.4 collective-permute-done.14
  296.8 2.0 collective-permute-start.15
  298.9 2.2 collective-permute-done.15
  301.1 79.7 %collective-permute-done.12 = f32[1,128,4,128]{3,1,2,0:T(8,128)S(1)} collective-permute-done((f32[1,128,4,128]{3,1,2,0:T(8,128)S(1)}, f32[1,128,4,128]{3,1,2,0:T(8,128)S(1)}, u32[]{:S(2)}, u32[]{:S(2)}) %collective-permute-start.12) | collective-permute-done | bytes 262176 | tf_op jit(solution)/shard_map/ppermute | solution.py:17
  380.8 1.3 copy-done.2
  382.1 33.5 %fusion.16 = f32[32,128,4,128]{3,1,2,0:T(8,128)} fusion(f32[32,128,4,128]{3,1,2,0:T(8,128)} %fusion.27, f32[32,128,1,128]{3,1,2,0:T(8,128)} %collective-permute-done.17, f32[34,1,4,128]{3,1,2,0:T(1,128)S(1)} %pad.59, f32[34,1,4,128]{3,1,2,0:T(1,128)S(1)} %pad.58, f32[1,128,4,128]{3,1,2,0:T(8,128)S(1)} %collective-permute-done.13, ...), kind=kLoop, calls=%fused_computation.35 | loop fusion | flops 71303168 | bytes 38412288 | tf_op jit(solution)/shard_map/add | solution.py:64
  415.6 2.5 fusion.49
  418.1 0.9 collective-permute-start.22
  419.0 3.7 collective-permute-start.23
  422.7 1.1 fusion.51
  423.8 0.1 collective-permute-start.18
  423.8 3.2 collective-permute-start.19
  427.1 1.3 fusion.50
  428.4 2.0 collective-permute-start.20
  430.4 4.4 collective-permute-done.20
  434.8 2.0 collective-permute-start.21
  436.9 2.2 collective-permute-done.21
  439.1 75.8 %collective-permute-done.18 = f32[1,128,4,128]{3,1,2,0:T(8,128)S(1)} collective-permute-done((f32[1,128,4,128]{3,1,2,0:T(8,128)S(1)}, f32[1,128,4,128]{3,1,2,0:T(8,128)S(1)}, u32[]{:S(2)}, u32[]{:S(2)}) %collective-permute-start.18) | collective-permute-done | bytes 262176 | tf_op jit(solution)/shard_map/ppermute | solution.py:17
  515.0 36.4 %add_reduce_fusion = (f32[32,4,128]{2,1,0:T(4,128)S(1)}, f32[32,4,128]{2,1,0:T(4,128)S(1)}, f32[32,128,4,128]{3,1,2,0:T(8,128)}) fusion(f32[32,128,4,128]{3,2,1,0:T(4,128)} %param.5, f32[32,128,4,128]{3,1,2,0:T(8,128)} %fusion.16, f32[32,128,1,128]{3,1,2,0:T(8,128)S(1)} %collective-permute-done.23, f32[34,1,4,128]{3,1,2,0:T(1,128)S(1)} %pad.63, ...), kind=kLoop, calls=%fused_computation.112 | loop fusion | flops 79659008 | bytes 38543360 | tf_op jit(solution)/shard_map/reduce_sum | solution.py:75
  551.4 1.1 broadcast_in_dim.3
  552.5 5.5 all-to-all-start
  558.0 14.0 %copy.68 = f32[32,128,4,128]{3,2,1,0:T(4,128)} copy(f32[32,128,4,128]{3,1,2,0:T(8,128)} %get-tuple-element.10) | data formatting | bytes 16777216
  571.9 0.5 reduce_sum.29
  572.4 8.7 %subtract_multiply_fusion = f32[32,128,4,128]{3,1,2,0:T(8,128)} fusion(f32[32,128,4,128]{3,1,2,0:T(8,128)} %get-tuple-element.10, f32[32,4,128]{2,1,0:T(4,128)S(1)} %bitcast.9, f32[32,4,128]{2,1,0:T(4,128)S(1)} %bitcast.8), kind=kLoop, calls=%fused_computation.110 | loop fusion | flops 4194304 | bytes 16908288 | tf_op jit(solution)/shard_map/mul | solution.py:83
  581.1 14.2 %copy.67 = f32[32,128,4,128]{3,2,1,0:T(4,128)} copy(f32[32,128,4,128]{3,1,2,0:T(8,128)} %subtract_multiply_fusion) | data formatting | bytes 16777216
  (32 shorter events, 0.5 us)
Async XLA Ops:
  5.3 108.8 %copy-start = (f32[32,128,4,128]{3,1,2,0:T(8,128)}, f32[32,128,4,128]{3,1,2,0:T(8,128)S(1)}, u32[]{:S(2)}) copy-start(f32[32,128,4,128]{3,1,2,0:T(8,128)S(1)} %copy.58) | copy-start | bytes 25165828
  5.8 109.1 %collective-permute-start.4 = (f32[32,128,1,128]{3,1,2,0:T(8,128)S(1)}, f32[32,128,1,128]{3,1,2,0:T(8,128)}, u32[]{:S(2)}, u32[]{:S(2)}) collective-permute-start(f32[32,128,1,128]{3,1,2,0:T(8,128)S(1)} %get-tuple-element.29), channel_id=1, source_target_pairs={{0,1},{1,2},{2,3},{3,4},{4,5},{5,6},{6,7},{7,0},{8,9},{9,10},{10,1... | collective-permute-start | bytes 6291464 | tf_op jit(solution)/shard_map/ppermute | solution.py:17
  7.5 107.4 %collective-permute-start.5 = (f32[32,128,1,128]{3,1,2,0:T(8,128)S(1)}, f32[32,128,1,128]{3,1,2,0:T(8,128)}, u32[]{:S(2)}, u32[]{:S(2)}) collective-permute-start(f32[32,128,1,128]{3,1,2,0:T(8,128)S(1)} %get-tuple-element.30), channel_id=1, source_target_pairs={{1,0},{2,1},{3,2},{4,3},{5,4},{6,5},{7,6},{0,7},{9,8},{10,9},{11,1... | collective-permute-start | bytes 6291464 | tf_op jit(solution)/shard_map/ppermute | solution.py:18
  10.0 94.9 %collective-permute-start = (f32[1,128,4,128]{3,1,2,0:T(8,128)S(1)}, f32[1,128,4,128]{3,1,2,0:T(8,128)S(1)}, u32[]{:S(2)}, u32[]{:S(2)}) collective-permute-start(f32[1,128,4,128]{3,1,2,0:T(8,128)S(1)} %get-tuple-element.34), channel_id=1, source_target_pairs={{0,32},{32,64},{64,96},{96,0},{1,33},{33,65},{65,97},{97,1},{2,34}... | collective-permute-start | bytes 786440 | tf_op jit(solution)/shard_map/ppermute | solution.py:17
  10.2 6.5 %collective-permute-start.2 = (f32[32,1,4,128]{3,1,2,0:T(1,128)S(1)}, f32[32,1,4,128]{3,1,2,0:T(1,128)S(1)}, u32[]{:S(2)}, u32[]{:S(2)}) collective-permute-start(f32[32,1,4,128]{3,1,2,0:T(1,128)S(1)} %get-tuple-element.31), channel_id=1, source_target_pairs={{0,8},{8,16},{16,24},{24,0},{1,9},{9,17},{17,25},{25,1},{2,10},{10... | collective-permute-start | bytes 196616 | tf_op jit(solution)/shard_map/ppermute | solution.py:17
  12.3 7.8 %collective-permute-start.3 = (f32[32,1,4,128]{3,1,2,0:T(1,128)S(1)}, f32[32,1,4,128]{3,1,2,0:T(1,128)S(1)}, u32[]{:S(2)}, u32[]{:S(2)}) collective-permute-start(f32[32,1,4,128]{3,1,2,0:T(1,128)S(1)} %get-tuple-element.32), channel_id=1, source_target_pairs={{8,0},{16,8},{24,16},{0,24},{9,1},{17,9},{25,17},{1,25},{10,2},{18... | collective-permute-start | bytes 196616 | tf_op jit(solution)/shard_map/ppermute | solution.py:18
  16.7 97.4 %collective-permute-start.1 = (f32[1,128,4,128]{3,1,2,0:T(8,128)S(1)}, f32[1,128,4,128]{3,1,2,0:T(8,128)S(1)}, u32[]{:S(2)}, u32[]{:S(2)}) collective-permute-start(f32[1,128,4,128]{3,1,2,0:T(8,128)S(1)} %get-tuple-element.33), channel_id=1, source_target_pairs={{32,0},{64,32},{96,64},{0,96},{33,1},{65,33},{97,65},{1,97},{34,2}... | collective-permute-start | bytes 786440 | tf_op jit(solution)/shard_map/ppermute | solution.py:18
  105.0 9.9 %slice-start = ((s8[8388608]{0:T(1024)(128)(4,1)}), s8[4194304]{0:T(1024)(128)(4,1)S(1)}, s32[]{:S(2)}) async-start(s8[8388608]{0:T(1024)(128)(4,1)} %bitcast.4), calls=%async_computation.1 | async-start | bytes 8388608
  105.7 9.2 %slice-start.1 = ((s8[8388608]{0:T(1024)(128)(4,1)}), s8[4194304]{0:T(1024)(128)(4,1)S(1)}, s32[]{:S(2)}) async-start(s8[8388608]{0:T(1024)(128)(4,1)} %bitcast.4), calls=%async_computation.2 | async-start | bytes 8388608
  148.1 95.2 %collective-permute-start.10 = (f32[32,128,1,128]{3,1,2,0:T(8,128)S(1)}, f32[32,128,1,128]{3,1,2,0:T(8,128)S(1)}, u32[]{:S(2)}, u32[]{:S(2)}) collective-permute-start(f32[32,128,1,128]{3,1,2,0:T(8,128)S(1)} %get-tuple-element.23), channel_id=1, source_target_pairs={{0,1},{1,2},{2,3},{3,4},{4,5},{5,6},{6,7},{7,0},{8,9},{9,10},{10,1... | collective-permute-start | bytes 6291464 | tf_op jit(solution)/shard_map/ppermute | solution.py:17
  149.4 95.3 %collective-permute-start.11 = (f32[32,128,1,128]{3,1,2,0:T(8,128)S(1)}, f32[32,128,1,128]{3,1,2,0:T(8,128)}, u32[]{:S(2)}, u32[]{:S(2)}) collective-permute-start(f32[32,128,1,128]{3,1,2,0:T(8,128)S(1)} %get-tuple-element.24), channel_id=1, source_target_pairs={{1,0},{2,1},{3,2},{4,3},{5,4},{6,5},{7,6},{0,7},{9,8},{10,9},{11,1... | collective-permute-start | bytes 6291464 | tf_op jit(solution)/shard_map/ppermute | solution.py:18
  153.4 89.9 %collective-permute-start.6 = (f32[1,128,4,128]{3,1,2,0:T(8,128)S(1)}, f32[1,128,4,128]{3,1,2,0:T(8,128)S(1)}, u32[]{:S(2)}, u32[]{:S(2)}) collective-permute-start(f32[1,128,4,128]{3,1,2,0:T(8,128)S(1)} %get-tuple-element.25), channel_id=1, source_target_pairs={{0,32},{32,64},{64,96},{96,0},{1,33},{33,65},{65,97},{97,1},{2,34}... | collective-permute-start | bytes 786440 | tf_op jit(solution)/shard_map/ppermute | solution.py:17
  153.5 89.9 %collective-permute-start.7 = (f32[1,128,4,128]{3,1,2,0:T(8,128)S(1)}, f32[1,128,4,128]{3,1,2,0:T(8,128)S(1)}, u32[]{:S(2)}, u32[]{:S(2)}) collective-permute-start(f32[1,128,4,128]{3,1,2,0:T(8,128)S(1)} %get-tuple-element.26), channel_id=1, source_target_pairs={{32,0},{64,32},{96,64},{0,96},{33,1},{65,33},{97,65},{1,97},{34,2}... | collective-permute-start | bytes 786440 | tf_op jit(solution)/shard_map/ppermute | solution.py:18
  158.0 6.4 %collective-permute-start.8 = (f32[32,1,4,128]{3,1,2,0:T(1,128)S(1)}, f32[32,1,4,128]{3,1,2,0:T(1,128)S(1)}, u32[]{:S(2)}, u32[]{:S(2)}) collective-permute-start(f32[32,1,4,128]{3,1,2,0:T(1,128)S(1)} %get-tuple-element.27), channel_id=1, source_target_pairs={{0,8},{8,16},{16,24},{24,0},{1,9},{9,17},{17,25},{25,1},{2,10},{10... | collective-permute-start | bytes 196616 | tf_op jit(solution)/shard_map/ppermute | solution.py:17
  164.4 4.5 collective-permute-start.9
  243.3 1.3 copy-start.1
  280.5 100.3 %collective-permute-start.16 = (f32[32,128,1,128]{3,1,2,0:T(8,128)S(1)}, f32[32,128,1,128]{3,1,2,0:T(8,128)S(1)}, u32[]{:S(2)}, u32[]{:S(2)}) collective-permute-start(f32[32,128,1,128]{3,1,2,0:T(8,128)S(1)} %get-tuple-element.17), channel_id=1, source_target_pairs={{0,1},{1,2},{2,3},{3,4},{4,5},{5,6},{6,7},{7,0},{8,9},{9,10},{10,1... | collective-permute-start | bytes 6291464 | tf_op jit(solution)/shard_map/ppermute | solution.py:17
  281.5 100.6 %collective-permute-start.17 = (f32[32,128,1,128]{3,1,2,0:T(8,128)S(1)}, f32[32,128,1,128]{3,1,2,0:T(8,128)}, u32[]{:S(2)}, u32[]{:S(2)}) collective-permute-start(f32[32,128,1,128]{3,1,2,0:T(8,128)S(1)} %get-tuple-element.18), channel_id=1, source_target_pairs={{1,0},{2,1},{3,2},{4,3},{5,4},{6,5},{7,6},{0,7},{9,8},{10,9},{11,1... | collective-permute-start | bytes 6291464 | tf_op jit(solution)/shard_map/ppermute | solution.py:18
  285.8 95.0 %collective-permute-start.12 = (f32[1,128,4,128]{3,1,2,0:T(8,128)S(1)}, f32[1,128,4,128]{3,1,2,0:T(8,128)S(1)}, u32[]{:S(2)}, u32[]{:S(2)}) collective-permute-start(f32[1,128,4,128]{3,1,2,0:T(8,128)S(1)} %get-tuple-element.19), channel_id=1, source_target_pairs={{0,32},{32,64},{64,96},{96,0},{1,33},{33,65},{65,97},{97,1},{2,34}... | collective-permute-start | bytes 786440 | tf_op jit(solution)/shard_map/ppermute | solution.py:17
  287.6 93.2 %collective-permute-start.13 = (f32[1,128,4,128]{3,1,2,0:T(8,128)S(1)}, f32[1,128,4,128]{3,1,2,0:T(8,128)S(1)}, u32[]{:S(2)}, u32[]{:S(2)}) collective-permute-start(f32[1,128,4,128]{3,1,2,0:T(8,128)S(1)} %get-tuple-element.20), channel_id=1, source_target_pairs={{32,0},{64,32},{96,64},{0,96},{33,1},{65,33},{97,65},{1,97},{34,2}... | collective-permute-start | bytes 786440 | tf_op jit(solution)/shard_map/ppermute | solution.py:18
  290.4 6.4 %collective-permute-start.14 = (f32[32,1,4,128]{3,1,2,0:T(1,128)S(1)}, f32[32,1,4,128]{3,1,2,0:T(1,128)S(1)}, u32[]{:S(2)}, u32[]{:S(2)}) collective-permute-start(f32[32,1,4,128]{3,1,2,0:T(1,128)S(1)} %get-tuple-element.21), channel_id=1, source_target_pairs={{0,8},{8,16},{16,24},{24,0},{1,9},{9,17},{17,25},{25,1},{2,10},{10... | collective-permute-start | bytes 196616 | tf_op jit(solution)/shard_map/ppermute | solution.py:17
  296.8 4.3 collective-permute-start.15
  380.8 1.3 copy-start.2
  418.1 96.9 %collective-permute-start.22 = (f32[32,128,1,128]{3,1,2,0:T(8,128)S(1)}, f32[32,128,1,128]{3,1,2,0:T(8,128)S(1)}, u32[]{:S(2)}, u32[]{:S(2)}) collective-permute-start(f32[32,128,1,128]{3,1,2,0:T(8,128)S(1)} %get-tuple-element.11), channel_id=1, source_target_pairs={{0,1},{1,2},{2,3},{3,4},{4,5},{5,6},{6,7},{7,0},{8,9},{9,10},{10,1... | collective-permute-start | bytes 6291464 | tf_op jit(solution)/shard_map/ppermute | solution.py:17
  419.0 95.9 %collective-permute-start.23 = (f32[32,128,1,128]{3,1,2,0:T(8,128)S(1)}, f32[32,128,1,128]{3,1,2,0:T(8,128)S(1)}, u32[]{:S(2)}, u32[]{:S(2)}) collective-permute-start(f32[32,128,1,128]{3,1,2,0:T(8,128)S(1)} %get-tuple-element.12), channel_id=1, source_target_pairs={{1,0},{2,1},{3,2},{4,3},{5,4},{6,5},{7,6},{0,7},{9,8},{10,9},{11,1... | collective-permute-start | bytes 6291464 | tf_op jit(solution)/shard_map/ppermute | solution.py:18
  423.8 91.2 %collective-permute-start.18 = (f32[1,128,4,128]{3,1,2,0:T(8,128)S(1)}, f32[1,128,4,128]{3,1,2,0:T(8,128)S(1)}, u32[]{:S(2)}, u32[]{:S(2)}) collective-permute-start(f32[1,128,4,128]{3,1,2,0:T(8,128)S(1)} %get-tuple-element.15), channel_id=1, source_target_pairs={{0,32},{32,64},{64,96},{96,0},{1,33},{33,65},{65,97},{97,1},{2,34}... | collective-permute-start | bytes 786440 | tf_op jit(solution)/shard_map/ppermute | solution.py:17
  423.8 91.1 %collective-permute-start.19 = (f32[1,128,4,128]{3,1,2,0:T(8,128)S(1)}, f32[1,128,4,128]{3,1,2,0:T(8,128)S(1)}, u32[]{:S(2)}, u32[]{:S(2)}) collective-permute-start(f32[1,128,4,128]{3,1,2,0:T(8,128)S(1)} %get-tuple-element.16), channel_id=1, source_target_pairs={{32,0},{64,32},{96,64},{0,96},{33,1},{65,33},{97,65},{1,97},{34,2}... | collective-permute-start | bytes 786440 | tf_op jit(solution)/shard_map/ppermute | solution.py:18
  428.4 6.4 %collective-permute-start.20 = (f32[32,1,4,128]{3,1,2,0:T(1,128)S(1)}, f32[32,1,4,128]{3,1,2,0:T(1,128)S(1)}, u32[]{:S(2)}, u32[]{:S(2)}) collective-permute-start(f32[32,1,4,128]{3,1,2,0:T(1,128)S(1)} %get-tuple-element.13), channel_id=1, source_target_pairs={{0,8},{8,16},{16,24},{24,0},{1,9},{9,17},{17,25},{25,1},{2,10},{10... | collective-permute-start | bytes 196616 | tf_op jit(solution)/shard_map/ppermute | solution.py:17
  434.8 4.3 collective-permute-start.21
  552.5 19.4 %all-to-all-start = ((f32[4,1,32768]{2,1,0:T(1,128)}), f32[4,1,32768]{2,1,0:T(1,128)S(1)}, u32[]{:S(2)}, u32[]{:S(2)}) async-start(f32[4,1,32768]{2,1,0:T(1,128)} %broadcast_in_dim.3), calls=%async_computation | async-start | bytes 1048576 | tf_op jit(solution)/shard_map/all_to_all | solution.py:31
where the time goes:
time: 606 us; the launch traced here: 595 us
  waiting for transfers between devices  337 us (56%)
  other arithmetic  143 us (24%)
  local copies, waits for them, and re-layouts  62 us (10%)
  starting transfers between devices  52.6 us (9%)
    ppermute x12, waiting for transfers between devices, padded(): lax.ppermute(last, axis, up)  330 us
    add x3, other arithmetic, march_forward(): return middle + diffusivity_ratio * spread + forcing_term  97.5 us
    unnamed x15, local copies, waits for them, and re-layouts  44.6 us
    reduce_sum x1, other arithmetic, local(): jnp.sum(moved, axis=1, keepdims=True)  36.4 us
    ppermute x12, starting transfers between devices, padded(): lax.ppermute(first, axis, [(b, a) for a, b in up])  32.2 us
    slice x11, local copies, waits for them, and re-layouts, padded(): last = lax.slice_in_dim(x, length - width, length, axis=dim)  15.2 us
    ppermute x12, starting transfers between devices, padded(): lax.ppermute(last, axis, up)  14.9 us
  transfers between devices with their start and end apart: 25, of which 11 were waited for; matrix products, arithmetic and copies ran while one was open for 5% of the time, Pallas kernels for 0%

commit v1 on v0

v1 whole, which is shorter than its diff:
```python
import functools

import jax
import jax.numpy as jnp
from jax import lax
from jax.experimental import pallas as pl
from jax.experimental.pallas import tpu as pltpu
from jax.sharding import PartitionSpec as P

STEPS = 4
CHUNKS = 8
MESH = pl.DeviceIdType.MESH


def kernel(
    sizes,
    heat_hbm,
    ratio_hbm,
    force_hbm,
    score,
    final,
    u,
    ratio,
    force,
    lon_out,
    lon_in,
    stat_out,
    stat_in,
    load_sem,
    lev_send,
    lev_recv,
    lon_send,
    lon_recv,
    lat_send,
    lat_recv,
    stat_send,
    stat_recv,
):
    lat_size, lon_size, lev_size = sizes
    rows, wide, height = u.shape[2] - 2, u.shape[3], u.shape[1] - 2
    per = rows // CHUNKS
    lat, lon, lev = (lax.axis_index(a) for a in ("lat", "lon", "lev"))
    after = {
        "lat": lax.rem(lat + 1, lat_size),
        "lon": lax.rem(lon + 1, lon_size),
        "lev": lax.rem(lev + 1, lev_size),
    }
    before = {
        "lat": lax.rem(lat + lat_size - 1, lat_size),
        "lon": lax.rem(lon + lon_size - 1, lon_size),
        "lev": lax.rem(lev + lev_size - 1, lev_size),
    }
    first_cell = lax.broadcasted_iota(jnp.int32, (wide, 128), 0) == 0
    last_cell = lax.broadcasted_iota(jnp.int32, (wide, 128), 0) == wide - 1

    def chunk_rows(c, offset=0):
        return pl.ds(c * per + offset, per)

    def load(i, c):
        src = (heat_hbm, ratio_hbm, force_hbm)[i]
        dst = (score, ratio, force)[i]
        return pltpu.make_async_copy(
            src.at[chunk_rows(c)], dst.at[chunk_rows(c)], load_sem.at[i, c]
        )

    def target(axis, d):
        return {axis: (before, after)[d][axis]}

    def lev_copy(p, d, c):
        src, dst = ((1, height + 1), (height, 0))[d]
        return pltpu.make_async_remote_copy(
            src_ref=u.at[p, src, chunk_rows(c, 1)],
            dst_ref=u.at[p, dst, chunk_rows(c, 1)],
            send_sem=lev_send.at[p, d, c],
            recv_sem=lev_recv.at[p, d, c],
            device_id=target("lev", d),
            device_id_type=MESH,
        )

    def lat_copy(p, d):
        src, dst = ((1, rows + 1), (rows, 0))[d]
        return pltpu.make_async_remote_copy(
            src_ref=u.at[p, pl.ds(1, height), src],
            dst_ref=u.at[p, pl.ds(1, height), dst],
            send_sem=lat_send.at[p, d],
            recv_sem=lat_recv.at[p, d],
            device_id=target("lat", d),
            device_id_type=MESH,
        )

    def lon_copy(p, d, c):
        return pltpu.make_async_remote_copy(
            src_ref=lon_out.at[p, d, chunk_rows(c)],
            dst_ref=lon_in.at[p, d, chunk_rows(c)],
            send_sem=lon_send.at[p, d, c],
            recv_sem=lon_recv.at[p, d, c],
            device_id=target("lon", d),
            device_id_type=MESH,
        )

    def stat_copy(j, c):
        return pltpu.make_async_remote_copy(
            src_ref=stat_out.at[chunk_rows(c)],
            dst_ref=stat_in.at[j, chunk_rows(c)],
            send_sem=stat_send.at[j, c],
            recv_sem=stat_recv.at[j, c],
            device_id={"lon": lax.rem(lon + j + 1, lon_size)},
            device_id_type=MESH,
        )

    def order(k):
        return lax.rem(k + CHUNKS - 1, CHUNKS)

    def on_edges(c, low, high):
        pl.when(c == 0)(low)
        pl.when(c == CHUNKS - 1)(high)

    def send_faces(p, c):
        on_edges(c, lambda: lat_copy(p, 0).start(), lambda: lat_copy(p, 1).start())
        for d in (0, 1):
            lev_copy(p, d, c).start()
        for d in (0, 1):
            lon_copy(p, d, c).start()

    def wait_sent(p, c):
        on_edges(c, lambda: lat_copy(p, 0).wait_send(), lambda: lat_copy(p, 1).wait_send())
        for d in (0, 1):
            lev_copy(p, d, c).wait_send()
            lon_copy(p, d, c).wait_send()

    def wait_faces(p, c):
        on_edges(c, lambda: lat_copy(p, 1).wait_recv(), lambda: lat_copy(p, 0).wait_recv())
        for d in (0, 1):
            lev_copy(p, d, c).wait_recv()
            lon_copy(p, d, c).wait_recv()

    def put(p, y, z, values):
        u[p, z + 1, y + 1] = values
        lon_out[p, 0, y, z] = values[0]
        lon_out[p, 1, y, z] = values[wide - 1]

    def cells(z):
        return pl.ds(z, wide, stride=height)

    def stepped(p, y, z):
        middle = u[p, z + 1, y + 1]
        west = jnp.where(first_cell, lon_in[p, 1, y, pl.ds(z, 1)], pltpu.roll(middle, 1, 0))
        east = jnp.where(last_cell, lon_in[p, 0, y, pl.ds(z, 1)], pltpu.roll(middle, wide - 1, 0))
        spread = (
            (u[p, z + 1, y] + u[p, z + 1, y + 2])
            + (west + east)
            + (u[p, z, y + 1] + u[p, z + 2, y + 1])
            - 6.0 * middle
        )
        return middle + ratio[y, cells(z)] * spread + force[y, cells(z)]

    def each_row(c, body):
        def one(i, carry):
            body(c * per + i)
            return carry

        lax.fori_loop(0, per, one, 0)

    def each_chunk(body):
        def one(k, carry):
            body(k, order(k))
            return carry

        lax.fori_loop(0, CHUNKS, one, 0)

    each_chunk(lambda k, c: load(0, c).start())
    for i in (1, 2):
        each_chunk(lambda k, c, i=i: load(i, c).start())

    barrier = pltpu.get_barrier_semaphore()
    greeted = [{a: n[a]} for a in ("lat", "lev") for n in (before, after)]
    greeted += [{"lon": lax.rem(lon + j + 1, lon_size)} for j in range(lon_size - 1)]
    for other in greeted:
        pl.semaphore_signal(barrier, inc=1, device_id=other, device_id_type=MESH)
    pl.semaphore_wait(barrier, len(greeted))

    def begin(k, c):
        load(0, c).wait()

        def one(y):
            for z in range(height):
                put(0, y, z, score[y, cells(z)])

        each_row(c, one)
        send_faces(0, c)

    each_chunk(begin)

    for step in range(1, STEPS):
        p, q = (step - 1) % 2, step % 2

        def advance(k, c, step=step, p=p, q=q):
            if step == 1:
                load(1, c).wait()
                load(2, c).wait()
            else:
                wait_sent(q, c)
            wait_faces(p, c)

            def one(y):
                for z in range(height):
                    put(q, y, z, stepped(p, y, z))

            each_row(c, one)
            send_faces(q, c)

        each_chunk(advance)

    p, q = (STEPS - 1) % 2, STEPS % 2

    def finish(c):
        for j in range(lon_size - 1):
            stat_copy(j, c).wait_recv()

        def one(y):
            own = stat_out[y]
            others = [stat_in[j, y] for j in range(lon_size - 1)]
            summed = own
            for other in others:
                summed = summed + other
            mean = summed[:height] / lon_size
            apart = (own[:height] - mean) * (own[:height] - mean)
            for other in others:
                apart = apart + (other[:height] - mean) * (other[:height] - mean)
            variance = summed[height:] / (lon_size * wide) + apart / lon_size
            scale = lax.rsqrt(variance + 0.0001)
            for z in range(height):
                score[y, cells(z)] = (u[q, z + 1, y + 1] - mean[z : z + 1]) * scale[z : z + 1]

        each_row(c, one)

    def last(k, c):
        wait_sent(q, c)
        wait_faces(p, c)

        def one(y):
            for z in range(height):
                values = stepped(p, y, z)
                u[q, z + 1, y + 1] = values
                final[y, cells(z)] = values
                mean = jnp.sum(values, axis=0, keepdims=True) / wide
                apart = values - mean
                stat_out[y, pl.ds(z, 1)] = mean
                stat_out[y, pl.ds(height + z, 1)] = jnp.sum(apart * apart, axis=0, keepdims=True)

        each_row(c, one)
        for j in range(lon_size - 1):
            stat_copy(j, c).start()
        pl.when(k > 0)(lambda: finish(order(k + CHUNKS - 1)))

    each_chunk(last)
    finish(order(CHUNKS - 1))

    def settle(k, c):
        wait_sent(p, c)
        for j in range(lon_size - 1):
            stat_copy(j, c).wait_send()

    each_chunk(settle)


def local(sizes, initial_heat, diffusivity_ratio, forcing_term):
    rows, wide, height, members = initial_heat.shape
    flat = (rows, wide * height, members)
    hbm = pl.BlockSpec(memory_space=pl.ANY)
    vmem = pl.BlockSpec(memory_space=pltpu.VMEM)
    f32, dma = jnp.float32, pltpu.SemaphoreType.DMA
    lon_size = sizes[1]
    score, final = pl.pallas_call(
        functools.partial(kernel, sizes),
        out_shape=(jax.ShapeDtypeStruct(flat, f32), jax.ShapeDtypeStruct(flat, f32)),
        in_specs=[hbm, hbm, hbm],
        out_specs=(vmem, vmem),
        scratch_shapes=[
            pltpu.VMEM((2, height + 2, rows + 2, wide, members), f32),
            pltpu.VMEM(flat, f32),
            pltpu.VMEM(flat, f32),
            pltpu.VMEM((2, 2, rows, height, members), f32),
            pltpu.VMEM((2, 2, rows, height, members), f32),
            pltpu.VMEM((rows, 2 * height, members), f32),
            pltpu.VMEM((lon_size - 1, rows, 2 * height, members), f32),
            dma((3, CHUNKS)),
            dma((2, 2, CHUNKS)),
            dma((2, 2, CHUNKS)),
            dma((2, 2, CHUNKS)),
            dma((2, 2, CHUNKS)),
            dma((2, 2)),
            dma((2, 2)),
            dma((lon_size - 1, CHUNKS)),
            dma((lon_size - 1, CHUNKS)),
        ],
        compiler_params=pltpu.CompilerParams(
            collective_id=0, has_side_effects=True, vmem_limit_bytes=63 * 2**20
        ),
    )(*(a.reshape(flat) for a in (initial_heat, diffusivity_ratio, forcing_term)))
    return score.reshape(initial_heat.shape), final.reshape(initial_heat.shape)


def solution(mesh):
    sizes = tuple(mesh.shape[a] for a in ("lat", "lon", "lev"))
    placed = P("lat", "lon", "lev", None)
    return jax.shard_map(
        functools.partial(local, sizes),
        mesh=mesh,
        in_specs=(placed, placed, placed),
        out_specs=(placed, placed),
        check_vma=False,
    )
```

time: 606 us -> 420 us (0.69); the launches traced: 595 us -> 420 us
  Pallas kernels: 0 us -> 404 us
  waiting for transfers between devices: 337 us -> 0 us
  other arithmetic: 143 us -> 0 us
  starting transfers between devices: 52.6 us -> 0 us
  local copies, waits for them, and re-layouts: 62 us -> 15.4 us
    pallas_call x0 -> x1, Pallas kernels: none -> 404 us  [local(): pl.pallas_call(functools.partial(kernel, sizes), out_shape=(jax.ShapeDtyp...]
    ppermute x24 -> x0, waiting for transfers between devices: 337 us -> none  [the longest x12 330 us: padded(): lax.ppermute(last, axis, up)]
    add x4 -> x0, other arithmetic: 97.6 us -> none  [the longest x3 97.5 us: march_forward(): return middle + diffusivity_ratio * spread + forcing_term]
    ppermute x24 -> x0, starting transfers between devices: 47.1 us -> none  [the longest x12 32.2 us: padded(): lax.ppermute(first, axis, [(b, a) for a, b in up])]
    reduce_sum x2 -> x0, other arithmetic: 36.9 us -> none  [the longest x1 36.4 us: local(): jnp.sum(moved, axis=1, keepdims=True)]
    unnamed x15 -> x2, local copies, waits for them, and re-layouts: 44.6 us -> 15.4 us
    slice x12 -> x0, local copies, waits for them, and re-layouts: 15.3 us -> none  [the longest x11 15.2 us: padded(): last = lax.slice_in_dim(x, length - width, length, axis=dim)]
    mul x1 -> x0, other arithmetic: 8.67 us -> none  [local(): deviations_from_mean * lax.rsqrt(line_variance + 0.0001)]
  transfers between devices with their start and end apart: 25 -> 0, of which waited for: 11 -> 0; matrix products, arithmetic and copies ran while one was open for 5% -> 0% of each run, Pallas kernels for 0% -> 0%
where the time goes in v1:
time: 420 us
  Pallas kernels  404 us (96%)
  local copies, waits for them, and re-layouts  15.4 us (4%)
    pallas_call x1, Pallas kernels, local(): pl.pallas_call(functools.partial(kernel, sizes), out_shape=(jax.ShapeDtyp...  404 us
    unnamed x2, local copies, waits for them, and re-layouts  15.4 us

profile of v1, /device:TPU:0, one launch (start us, length us, event | category | flops | bytes accessed | tf_op | source)
XLA Modules:
  0.0 420.1 jit_solution(8447216557791878411)
XLA Ops:
  0.6 404.1 %shard_map.50 = (f32[32,512,128]{2,1,0:T(8,128)}, f32[32,512,128]{2,1,0:T(8,128)}) custom-call(f32[32,512,128]{2,1,0:T(8,128)} %bitcast.5, f32[32,512,128]{2,1,0:T(8,128)} %bitcast.6, f32[32,512,128]{2,1,0:T(8,128)} %bitcast.7), custom_call_target="tpu_custom_call" | custom-call | tf_op jit(solution)/shard_map/pallas_call | solution.py:274
  404.8 7.7 %copy.7 = f32[32,128,4,128]{3,2,1,0:T(4,128)} copy(f32[32,128,4,128]{3,2,1,0:T(4,128)} %bitcast.9) | data formatting | bytes 16777216
  412.4 7.7 %copy.8 = f32[32,128,4,128]{3,2,1,0:T(4,128)} copy(f32[32,128,4,128]{3,2,1,0:T(4,128)} %bitcast.8) | data formatting | bytes 16777216

commit v2 on v1

--- a/solution.py
+++ b/solution.py
@@ -169,15 +169,12 @@
         lax.fori_loop(0, CHUNKS, one, 0)
 
     each_chunk(lambda k, c: load(0, c).start())
-    for i in (1, 2):
-        each_chunk(lambda k, c, i=i: load(i, c).start())
 
     barrier = pltpu.get_barrier_semaphore()
     greeted = [{a: n[a]} for a in ("lat", "lev") for n in (before, after)]
     greeted += [{"lon": lax.rem(lon + j + 1, lon_size)} for j in range(lon_size - 1)]
     for other in greeted:
         pl.semaphore_signal(barrier, inc=1, device_id=other, device_id_type=MESH)
-    pl.semaphore_wait(barrier, len(greeted))
 
     def begin(k, c):
         load(0, c).wait()
@@ -187,7 +184,10 @@
                 put(0, y, z, score[y, cells(z)])
 
         each_row(c, one)
+        pl.when(k == 0)(lambda: pl.semaphore_wait(barrier, len(greeted)))
         send_faces(0, c)
+        for i in (1, 2):
+            load(i, c).start()
 
     each_chunk(begin)
 
@@ -264,6 +264,17 @@
     each_chunk(settle)
 
 
+def write_out(score, final, score_hbm, final_hbm, sem):
+    copies = [
+        pltpu.make_async_copy(score, score_hbm, sem.at[0]),
+        pltpu.make_async_copy(final, final_hbm, sem.at[1]),
+    ]
+    for copy in copies:
+        copy.start()
+    for copy in copies:
+        copy.wait()
+
+
 def local(sizes, initial_heat, diffusivity_ratio, forcing_term):
     rows, wide, height, members = initial_heat.shape
     flat = (rows, wide * height, members)
@@ -273,7 +284,7 @@
     lon_size = sizes[1]
     score, final = pl.pallas_call(
         functools.partial(kernel, sizes),
-        out_shape=(jax.ShapeDtypeStruct(flat, f32), jax.ShapeDtypeStruct(flat, f32)),
+        out_shape=(pltpu.VMEM(flat, f32), pltpu.VMEM(flat, f32)),
         in_specs=[hbm, hbm, hbm],
         out_specs=(vmem, vmem),
         scratch_shapes=[
@@ -295,9 +306,17 @@
             dma((lon_size - 1, CHUNKS)),
         ],
         compiler_params=pltpu.CompilerParams(
-            collective_id=0, has_side_effects=True, vmem_limit_bytes=63 * 2**20
+            collective_id=0, has_side_effects=True, vmem_limit_bytes=46 * 2**20
         ),
     )(*(a.reshape(flat) for a in (initial_heat, diffusivity_ratio, forcing_term)))
+    score, final = pl.pallas_call(
+        write_out,
+        out_shape=(jax.ShapeDtypeStruct(flat, f32), jax.ShapeDtypeStruct(flat, f32)),
+        in_specs=[vmem, vmem],
+        out_specs=(hbm, hbm),
+        scratch_shapes=[dma((2,))],
+        compiler_params=pltpu.CompilerParams(vmem_limit_bytes=4 * 2**20),
+    )(*(pltpu.with_memory_space_constraint(a, pltpu.VMEM) for a in (score, final)))
     return score.reshape(initial_heat.shape), final.reshape(initial_heat.shape)
 
 

time: 420 us -> 405 us (0.964)
  local copies, waits for them, and re-layouts: 15.4 us -> 0 us
    unnamed x2 -> x0, local copies, waits for them, and re-layouts: 15.4 us -> none
    pallas_call x1 -> x2, Pallas kernels: 404 us -> 404 us  [the longest x1 398 us: local(): pl.pallas_call(functools.partial(kernel, sizes), out_shape=(pltpu.VMEM(fl...]
where the time goes in v2:
time: 405 us
  Pallas kernels  404 us (100%)
    pallas_call x1, Pallas kernels, local(): pl.pallas_call(functools.partial(kernel, sizes), out_shape=(pltpu.VMEM(fl...  398 us

profile of v2, /device:TPU:0, one launch (start us, length us, event | category | flops | bytes accessed | tf_op | source)
XLA Modules:
  0.0 405.0 jit_solution(8649308470249445065)
XLA Ops:
  0.6 398.2 %shard_map.50 = (f32[32,512,128]{2,1,0:T(8,128)S(1)}, f32[32,512,128]{2,1,0:T(8,128)S(1)}) custom-call(f32[32,512,128]{2,1,0:T(8,128)} %bitcast.5, f32[32,512,128]{2,1,0:T(8,128)} %bitcast.6, f32[32,512,128]{2,1,0:T(8,128)} %bitcast.7), custom_call_target="tpu_custom_call" | custom-call | tf_op jit(solution)/shard_map/pallas_call | solution.py:285
  398.8 6.2 %shard_map.51 = (f32[32,512,128]{2,1,0:T(8,128)}, f32[32,512,128]{2,1,0:T(8,128)}) custom-call(f32[32,512,128]{2,1,0:T(8,128)S(1)} %get-tuple-element.6.score, f32[32,512,128]{2,1,0:T(8,128)S(1)} %get-tuple-element.7.final), custom_call_target="tpu_custom_call" | custom-call | tf_op jit(solution)/shard_map/pallas_call | solution.py:312

commit v3 on v0

v3 whole, which is shorter than its diff:
```python
import functools

import jax
import jax.numpy as jnp
from jax import lax
from jax.experimental import pallas as pl
from jax.experimental.pallas import tpu as pltpu
from jax.sharding import PartitionSpec as P

STEPS = 4
DEPTH = 2
SLOTS = 2
PARTS = 8
MESH = pl.DeviceIdType.MESH


def kernel(
    sizes,
    heat_hbm,
    ratio_hbm,
    force_hbm,
    score,
    final,
    u,
    ratio,
    force,
    packed,
    lat_in,
    lat_held,
    lon_out,
    lon_in,
    stat_out,
    stat_in,
    moment_out,
    moment_in,
    load_sem,
    swap_send,
    swap_recv,
    back_send,
    back_recv,
    lev_send,
    lev_recv,
    lon_send,
    lon_recv,
    lat_send,
    lat_recv,
    stat_send,
    stat_recv,
    moment_send,
    moment_recv,
):
    lat_size, lon_size, lev_size = sizes
    rows = final.shape[0]
    chunks, slab, members = u.shape[2:]
    height = u.shape[1] - 2
    pairs = height // 2
    wide = slab // (2 * DEPTH)
    lines = 2 * DEPTH
    lat, lon, lev = (lax.axis_index(a) for a in ("lat", "lon", "lev"))
    kind = lax.rem(lev, 2)
    outer_x = lat // (lat_size // 2)
    half = lax.rem(kind + outer_x, 2)
    partner_lev = lev + 1 - 2 * kind

    lane = lax.broadcasted_iota(jnp.int32, (wide, members), 1)
    line = lax.broadcasted_iota(jnp.int32, (wide, members), 0)
    low_lanes = lane < members // 2
    first_cell = line == 0
    last_cell = line == wide - 1

    def lat_target(d):
        other = lax.rem(lat + (lat_size - 1, 1)[d], lat_size)
        crossed = lax.rem(other // (lat_size // 2) + outer_x, 2)
        return {"lat": other, "lev": lev + crossed * (1 - 2 * kind)}

    def lev_target(d):
        return {"lev": lax.rem(lev + (lev_size - 2, 2)[d], lev_size)}

    def lon_target(d):
        return {"lon": lax.rem(lon + (lon_size - 1, 1)[d], lon_size)}

    def stat_target(j):
        return {"lon": lax.rem(lon + j + 1, lon_size)}

    def swapped(x):
        return pltpu.roll(x, members // 2, 1)

    def butterfly(a, b):
        return jnp.where(low_lanes, a, swapped(b)), jnp.where(low_lanes, swapped(a), b)

    def remote(src, dst, send_sem, recv_sem, target):
        return pltpu.make_async_remote_copy(
            src_ref=src,
            dst_ref=dst,
            send_sem=send_sem,
            recv_sem=recv_sem,
            device_id=target,
            device_id_type=MESH,
        )

    def row_of(c, i, side):
        return c * DEPTH + i if side == 0 else rows - 1 - c * DEPTH - i

    def staged(c, f, side):
        return (lax.rem(c, 2) * 3 + f) * lines + side * DEPTH

    def load(f, c, side):
        src = (heat_hbm, ratio_hbm, force_hbm)[f]
        first = c * DEPTH if side == 0 else rows - (c + 1) * DEPTH
        return pltpu.make_async_copy(
            src.at[pl.ds(first, DEPTH)],
            final.at[pl.ds(staged(c, f, side), DEPTH)],
            load_sem.at[f, side, lax.rem(c, 2)],
        )

    def plane(f, z):
        return (u.at[0, 1 + z], ratio.at[z], force.at[z])[f]

    def swap_copy(f, i, c):
        slot = lax.rem(c, SLOTS)
        return remote(
            packed.at[slot, f, i],
            plane(f, 2 * i + kind).at[c],
            swap_send.at[slot, f, i],
            swap_recv.at[c, f, i],
            {"lev": partner_lev},
        )

    def back_copy(i, c):
        return remote(
            ratio.at[2 * i + 1 - kind, c],
            score.at[c * pairs + i],
            back_send.at[c, i],
            back_recv.at[c, i],
            {"lev": partner_lev},
        )

    def lev_copy(p, d, c):
        src, dst = ((1, height + 1), (height, 0))[d]
        return remote(
            u.at[p, src, c],
            u.at[p, dst, c],
            lev_send.at[p, d, c],
            lev_recv.at[p, d, c],
            lev_target(d),
        )

    def lat_copy(p, d):
        return remote(
            u.at[p, pl.ds(1, height), 0, pl.ds(d * wide, wide)],
            lat_in.at[p, 1 - d],
            lat_send.at[p, d],
            lat_recv.at[p, d],
            lat_target(d),
        )

    def lon_copy(p, d, c):
        return remote(
            lon_out.at[p, d, c],
            lon_in.at[p, d, c],
            lon_send.at[p, d, c],
            lon_recv.at[p, d, c],
            lon_target(d),
        )

    def stat_copy(j, c):
        return remote(
            stat_out.at[c],
            stat_in.at[j, c],
            stat_send.at[j, c],
            stat_recv.at[j, c],
            stat_target(j),
        )

    def at_edge(c, body):
        @pl.when(c == 0)
        def _():
            for d in (0, 1):
                body(d)

    def send_faces(p, c):
        at_edge(c, lambda d: lat_copy(p, d).start())
        for d in (0, 1):
            lev_copy(p, d, c).start()
        for d in (0, 1):
            lon_copy(p, d, c).start()

    def wait_sent(p, c):
        at_edge(c, lambda d: lat_copy(p, d).wait_send())
        for d in (0, 1):
            lev_copy(p, d, c).wait_send()
            lon_copy(p, d, c).wait_send()

    def wait_faces(p, c):
        at_edge(c, lambda d: lat_copy(p, d).wait_recv())
        for d in (0, 1):
            lev_copy(p, d, c).wait_recv()
            lon_copy(p, d, c).wait_recv()

    def of_line(q):
        return pl.ds(q * wide, wide)

    def cells(z):
        return pl.ds(z, wide, stride=height)

    def put(p, c, q, z, values):
        u[p, z + 1, c, of_line(q)] = values
        lon_out[p, 0, c, q * height + z] = values[0]
        lon_out[p, 1, c, q * height + z] = values[wide - 1]

    def stepped(p, c, q, z):
        i, side = q // 2, q % 2
        middle = u[p, z + 1, c, of_line(q)]
        if i == 0:
            before = u[p, z + 1, jnp.maximum(c - 1, 0), of_line(lines - 2 + side)]
            outside = jnp.where(c == 0, lat_held[side, z], before)
        else:
            outside = u[p, z + 1, c, of_line(q - 2)]
        if i == DEPTH - 1:
            end = c == chunks - 1
            at = jnp.where(end, (lines - 1 - side) * wide, side * wide)
            inside = u[
                p, z + 1, jnp.minimum(c + 1, chunks - 1), pl.ds(pl.multiple_of(at, wide), wide)
            ]
        else:
            inside = u[p, z + 1, c, of_line(q + 2)]
        low, high = u[p, z, c, of_line(q)], u[p, z + 2, c, of_line(q)]
        if z == 0:
            low = swapped(jnp.where(low_lanes, u[p, height, c, of_line(q)], low))
        if z == height - 1:
            high = swapped(jnp.where(low_lanes, high, u[p, 1, c, of_line(q)]))
        at = pl.ds(q * height + z, 1)
        west = jnp.where(first_cell, lon_in[p, 1, c, at], pltpu.roll(middle, 1, 0))
        east = jnp.where(last_cell, lon_in[p, 0, c, at], pltpu.roll(middle, wide - 1, 0))
        spread = (outside + inside) + (west + east) + (low + high) - 6.0 * middle
        return middle + ratio[z, c, of_line(q)] * spread + force[z, c, of_line(q)]

    def start_loads(c):
        for f in range(3):
            for side in (0, 1):
                load(f, c, side).start()

    barrier = pltpu.get_barrier_semaphore()
    greeted = [{"lev": partner_lev}]
    greeted += [t(d) for t in (lat_target, lev_target) for d in (0, 1)]
    greeted += [stat_target(j) for j in range(lon_size - 1)]

    def pack(f, n, c):
        slot = lax.rem(c, SLOTS)
        for q in range(lines):
            i, side = q // 2, q % 2
            row = staged(c, f, side) + (i if side == 0 else DEPTH - 1 - i)
            a, b = butterfly(final[row, cells(2 * n)], final[row, cells(2 * n + 1)])
            plane(f, 2 * n + kind)[c, of_line(q)] = jnp.where(half == 0, a, b)
            packed[slot, f, n, of_line(q)] = jnp.where(half == 0, b, a)

    def pack_all(c, meet=False):
        for f in range(3):
            for side in (0, 1):
                load(f, c, side).wait()
            for n in range(pairs):
                pack(f, n, c)
                if meet and f == 0 and n == 0:
                    pl.semaphore_wait(barrier, len(greeted))
                swap_copy(f, n, c).start()

    start_loads(0)
    for other in greeted:
        pl.semaphore_signal(barrier, inc=1, device_id=other, device_id_type=MESH)
    start_loads(1)
    pack_all(0, meet=True)
    start_loads(2)
    pack_all(1)
    start_loads(3)

    def arrange(c):
        for f in range(3):
            for n in range(pairs):
                swap_copy(f, n, c).wait_recv()
            for q in range(lines):
                for n in range(pairs):
                    at = of_line(q)
                    a, b = butterfly(plane(f, 2 * n)[c, at], plane(f, 2 * n + 1)[c, at])
                    if f == 0:
                        put(0, c, q, 2 * n, a)
                        put(0, c, q, 2 * n + 1, b)
                    else:
                        plane(f, 2 * n)[c, at] = a
                        plane(f, 2 * n + 1)[c, at] = b
            if f == 0:
                send_faces(0, c)

    def advance(s, c):
        p, q_ = (s - 1) % 2, s % 2
        if s >= 2:
            wait_sent(q_, c)
        wait_faces(p, c)

        @pl.when(c == 0)
        def _():
            lat_held[...] = lat_in[p]

        for q in range(lines):
            if s < STEPS:
                for z in range(height):
                    put(q_, c, q, z, stepped(p, c, q, z))
            else:
                for n in range(pairs):
                    a, b = butterfly(stepped(p, c, q, 2 * n), stepped(p, c, q, 2 * n + 1))
                    ratio[2 * n, c, of_line(q)] = a
                    ratio[2 * n + 1, c, of_line(q)] = b
        if s < STEPS:
            send_faces(q_, c)
        else:
            for n in range(pairs):
                back_copy(n, c).start()

    def wave(k, carry):
        @pl.when(k < chunks)
        def _():
            arrange(k)

        @pl.when(k + SLOTS < chunks)
        def _():
            c = k + SLOTS
            for f in range(3):
                for n in range(pairs):
                    swap_copy(f, n, c - SLOTS).wait_send()
            pack_all(c)

            @pl.when(c + 2 < chunks)
            def _():
                start_loads(c + 2)

        for s in range(1, STEPS + 1):

            @pl.when((k >= s) & (k < chunks + s))
            def _(s=s):
                advance(s, k - s)

        return carry

    lax.fori_loop(0, chunks + STEPS, wave, 0)

    def note(c, at, values):
        mean = jnp.sum(values, axis=0, keepdims=True) / wide
        apart = values - mean
        stat_out[c, pl.ds(at, 1)] = mean
        stat_out[c, pl.ds(at + height, 1)] = jnp.sum(apart * apart, axis=0, keepdims=True)

    def moments(c, q):
        at = pl.ds(2 * height * q, 2 * height)
        own = stat_out[c, at]
        others = [stat_in[j, c, at] for j in range(lon_size - 1)]
        summed = own
        for other in others:
            summed = summed + other
        mean = summed[:height] / lon_size
        apart = (own[:height] - mean) * (own[:height] - mean)
        for other in others:
            apart = apart + (other[:height] - mean) * (other[:height] - mean)
        variance = summed[height:] / (lon_size * wide) + apart / lon_size
        return mean, lax.rsqrt(variance + 0.0001)

    end = chunks - 1
    for q in range(lines):
        for z in range(height):
            note(end, 2 * height * q + z, ratio[z, end, of_line(q)])
    for j in range(lon_size - 1):
        stat_copy(j, end).start()

    def whole(c, q, n):
        own = ratio[2 * n + kind, c, of_line(q)]
        other = score[c * pairs + n, of_line(q)]
        return butterfly(jnp.where(half == 0, own, other), jnp.where(half == 0, other, own))

    def restore(c):
        for n in range(pairs):
            back_copy(n, c).wait_recv()
        for q in range(lines):
            row = row_of(c, q // 2, q % 2)
            for n in range(pairs):
                for z, values in zip((2 * n, 2 * n + 1), whole(c, q, n)):
                    final[row, cells(z)] = values
                    note(c, 2 * height * q + z, values)
        for j in range(lon_size - 1):
            stat_copy(j, c).start()

    def finish(c):
        for j in range(lon_size - 1):
            stat_copy(j, c).wait_recv()
        for q in range(lines):
            row = row_of(c, q // 2, q % 2)
            mean, scale = moments(c, q)
            for z in range(height):
                values = final[row, cells(z)]
                score[row, cells(z)] = (values - mean[z : z + 1]) * scale[z : z + 1]

    def share_moments():
        for j in range(lon_size - 1):
            stat_copy(j, end).wait_recv()
        for q in range(lines):
            mean, scale = moments(end, q)
            moment_out[q, pl.ds(0, height)] = mean
            moment_out[q, pl.ds(height, height)] = scale
        moment_copy.start()

    def last(c, carry):
        restore(c)
        pl.when(c > 0)(lambda: finish(c - 1))
        pl.when(c == 0)(share_moments)
        return carry

    moment_copy = remote(
        moment_out, moment_in, moment_send, moment_recv, {"lev": partner_lev}
    )
    lax.fori_loop(0, end, last, 0)
    finish(end - 1)

    moment_copy.wait_recv()

    def spread_out(own, other):
        a, b = jnp.where(half == 0, own, other), jnp.where(half == 0, other, own)
        first = lax.broadcasted_iota(jnp.int32, a.shape, 1) < members // 2
        return (
            jnp.where(first, a, pltpu.roll(b, members // 2, 1)),
            jnp.where(first, pltpu.roll(a, members // 2, 1), b),
        )

    for n in range(pairs):
        back_copy(n, end).wait_recv()
        for q in range(lines):
            row = row_of(end, q // 2, q % 2)
            for z, values in zip((2 * n, 2 * n + 1), whole(end, q, n)):
                final[row, cells(z)] = values
    for n in range(pairs):
        for q in range(lines):
            row = row_of(end, q // 2, q % 2)
            ours = 2 * n + kind
            means, scales = (
                spread_out(moment_out[q, pl.ds(o + ours, 1)], moment_in[q, pl.ds(o + ours, 1)])
                for o in (0, height)
            )
            for z, m, k in zip((2 * n, 2 * n + 1), means, scales):
                score[row, cells(z)] = (final[row, cells(z)] - m) * k

    def settle(c, carry):
        wait_sent((STEPS - 1) % 2, c)
        for n in range(pairs):
            back_copy(n, c).wait_send()
        for j in range(lon_size - 1):
            stat_copy(j, c).wait_send()
        return carry

    lax.fori_loop(0, chunks, settle, 0)
    moment_copy.wait_send()
    for c in range(chunks - SLOTS, chunks):
        for f in range(3):
            for n in range(pairs):
                swap_copy(f, n, c).wait_send()


def write_out(score, final, score_hbm, final_hbm, sem):
    rows = score.shape[0] // PARTS
    copies = [
        pltpu.make_async_copy(
            src.at[pl.ds(i * rows, rows)], dst.at[pl.ds(i * rows, rows)], sem.at[n, i]
        )
        for i in range(PARTS)
        for n, (src, dst) in enumerate(((score, score_hbm), (final, final_hbm)))
    ]
    for copy in copies:
        copy.start()
    for copy in copies:
        copy.wait()


def local(sizes, initial_heat, diffusivity_ratio, forcing_term):
    rows, wide, height, members = initial_heat.shape
    flat = (rows, wide * height, members)
    chunks, slab = rows // (2 * DEPTH), 2 * DEPTH * wide
    hbm = pl.BlockSpec(memory_space=pl.ANY)
    vmem = pl.BlockSpec(memory_space=pltpu.VMEM)
    f32, dma = jnp.float32, pltpu.SemaphoreType.DMA
    others, pairs = sizes[1] - 1, height // 2
    score, final = pl.pallas_call(
        functools.partial(kernel, sizes),
        out_shape=(pltpu.VMEM(flat, f32), pltpu.VMEM(flat, f32)),
        in_specs=[hbm, hbm, hbm],
        out_specs=(vmem, vmem),
        scratch_shapes=[
            pltpu.VMEM((2, height + 2, chunks, slab, members), f32),
            pltpu.VMEM((height, chunks, slab, members), f32),
            pltpu.VMEM((height, chunks, slab, members), f32),
            pltpu.VMEM((SLOTS, 3, pairs, slab, members), f32),
            pltpu.VMEM((2, 2, height, wide, members), f32),
            pltpu.VMEM((2, height, wide, members), f32),
            pltpu.VMEM((2, 2, chunks, 2 * DEPTH * height, members), f32),
            pltpu.VMEM((2, 2, chunks, 2 * DEPTH * height, members), f32),
            pltpu.VMEM((chunks, 4 * DEPTH * height, members), f32),
            pltpu.VMEM((others, chunks, 4 * DEPTH * height, members), f32),
            pltpu.VMEM((2 * DEPTH, 2 * height, members), f32),
            pltpu.VMEM((2 * DEPTH, 2 * height, members), f32),
            dma((3, 2, 2)),
            dma((SLOTS, 3, pairs)),
            dma((chunks, 3, pairs)),
            dma((chunks, pairs)),
            dma((chunks, pairs)),
            dma((2, 2, chunks)),
            dma((2, 2, chunks)),
            dma((2, 2, chunks)),
            dma((2, 2, chunks)),
            dma((2, 2)),
            dma((2, 2)),
            dma((others, chunks)),
            dma((others, chunks)),
            dma,
            dma,
        ],
        compiler_params=pltpu.CompilerParams(
            collective_id=0, has_side_effects=True, vmem_limit_bytes=int(47.25 * 2**20)
        ),
    )(*(a.reshape(flat) for a in (initial_heat, diffusivity_ratio, forcing_term)))
    score, final = pl.pallas_call(
        write_out,
        out_shape=(jax.ShapeDtypeStruct(flat, f32), jax.ShapeDtypeStruct(flat, f32)),
        in_specs=[vmem, vmem],
        out_specs=(hbm, hbm),
        scratch_shapes=[dma((2, PARTS))],
        compiler_params=pltpu.CompilerParams(vmem_limit_bytes=4 * 2**20),
    )(*(pltpu.with_memory_space_constraint(a, pltpu.VMEM) for a in (score, final)))
    return score.reshape(initial_heat.shape), final.reshape(initial_heat.shape)


def solution(mesh):
    sizes = tuple(mesh.shape[a] for a in ("lat", "lon", "lev"))
    placed = P("lat", "lon", "lev", None)
    return jax.shard_map(
        functools.partial(local, sizes),
        mesh=mesh,
        in_specs=(placed, placed, placed),
        out_specs=(placed, placed),
        check_vma=False,
    )
```

time: 606 us -> 376 us (0.62); the launches traced: 595 us -> 376 us
  Pallas kernels: 0 us -> 375 us
  waiting for transfers between devices: 337 us -> 0 us
  other arithmetic: 143 us -> 0 us
  local copies, waits for them, and re-layouts: 62 us -> 0 us
  starting transfers between devices: 52.6 us -> 0 us
    pallas_call x0 -> x2, Pallas kernels: none -> 375 us  [the longest x1 369 us: local(): pl.pallas_call(functools.partial(kernel, sizes), out_shape=(pltpu.VMEM(fl...]
    ppermute x24 -> x0, waiting for transfers between devices: 337 us -> none  [the longest x12 330 us: padded(): lax.ppermute(last, axis, up)]
    add x4 -> x0, other arithmetic: 97.6 us -> none  [the longest x3 97.5 us: march_forward(): return middle + diffusivity_ratio * spread + forcing_term]
    ppermute x24 -> x0, starting transfers between devices: 47.1 us -> none  [the longest x12 32.2 us: padded(): lax.ppermute(first, axis, [(b, a) for a, b in up])]
    unnamed x15 -> x0, local copies, waits for them, and re-layouts: 44.6 us -> none
    reduce_sum x2 -> x0, other arithmetic: 36.9 us -> none  [the longest x1 36.4 us: local(): jnp.sum(moved, axis=1, keepdims=True)]
    slice x12 -> x0, local copies, waits for them, and re-layouts: 15.3 us -> none  [the longest x11 15.2 us: padded(): last = lax.slice_in_dim(x, length - width, length, axis=dim)]
    mul x1 -> x0, other arithmetic: 8.67 us -> none  [local(): deviations_from_mean * lax.rsqrt(line_variance + 0.0001)]
  transfers between devices with their start and end apart: 25 -> 0, of which waited for: 11 -> 0; matrix products, arithmetic and copies ran while one was open for 5% -> 0% of each run, Pallas kernels for 0% -> 0%
where the time goes in v3:
time: 376 us
  Pallas kernels  375 us (100%)
    pallas_call x1, Pallas kernels, local(): pl.pallas_call(functools.partial(kernel, sizes), out_shape=(pltpu.VMEM(fl...  369 us

profile of v3, /device:TPU:0, one launch (start us, length us, event | category | flops | bytes accessed | tf_op | source)
XLA Modules:
  0.0 376.0 jit_solution(3096049822876263037)
XLA Ops:
  0.6 369.4 %shard_map.50 = (f32[32,512,128]{2,1,0:T(8,128)S(1)}, f32[32,512,128]{2,1,0:T(8,128)S(1)}) custom-call(f32[32,512,128]{2,1,0:T(8,128)} %bitcast.5, f32[32,512,128]{2,1,0:T(8,128)} %bitcast.6, f32[32,512,128]{2,1,0:T(8,128)} %bitcast.7), custom_call_target="tpu_custom_call" | custom-call | tf_op jit(solution)/shard_map/pallas_call | solution.py:486
  370.1 6.0 %shard_map.51 = (f32[32,512,128]{2,1,0:T(8,128)}, f32[32,512,128]{2,1,0:T(8,128)}) custom-call(f32[32,512,128]{2,1,0:T(8,128)S(1)} %get-tuple-element.6.score, f32[32,512,128]{2,1,0:T(8,128)S(1)} %get-tuple-element.7.final), custom_call_target="tpu_custom_call" | custom-call | tf_op jit(solution)/shard_map/pallas_call | solution.py:524

commit v4 on v3

--- a/solution.py
+++ b/solution.py
@@ -48,6 +48,7 @@
     stat_recv,
     moment_send,
     moment_recv,
+    met,
 ):
     lat_size, lon_size, lev_size = sizes
     rows = final.shape[0]
@@ -113,25 +114,32 @@
             load_sem.at[f, side, lax.rem(c, 2)],
         )
 
-    def plane(f, z):
-        return (u.at[0, 1 + z], ratio.at[z], force.at[z])[f]
-
-    def swap_copy(f, i, c):
+    def place(z):
+        return z // 2 + (z % 2) * pairs
+
+    def planes(f, first, count):
+        return (u.at[0, pl.ds(1 + first, count)], ratio.at[pl.ds(first, count)], force.at[pl.ds(first, count)])[f]
+
+    def plane(f, n):
+        return (u.at[0, 1 + n], ratio.at[n], force.at[n])[f]
+
+    def swap_copy(f, c, at=None):
         slot = lax.rem(c, SLOTS)
+        at = pl.ds(0, slab) if at is None else at
         return remote(
-            packed.at[slot, f, i],
-            plane(f, 2 * i + kind).at[c],
-            swap_send.at[slot, f, i],
-            swap_recv.at[c, f, i],
+            packed.at[slot, f, :, at],
+            planes(f, kind * pairs, pairs).at[:, c, at],
+            swap_send.at[slot, f],
+            swap_recv.at[c, f],
             {"lev": partner_lev},
         )
 
-    def back_copy(i, c):
+    def back_copy(c):
         return remote(
-            ratio.at[2 * i + 1 - kind, c],
-            score.at[c * pairs + i],
-            back_send.at[c, i],
-            back_recv.at[c, i],
+            ratio.at[pl.ds((1 - kind) * pairs, pairs), c],
+            score.at[pl.ds(c * pairs, pairs)],
+            back_send.at[c],
+            back_recv.at[c],
             {"lev": partner_lev},
         )
 
@@ -204,36 +212,41 @@
         return pl.ds(z, wide, stride=height)
 
     def put(p, c, q, z, values):
-        u[p, z + 1, c, of_line(q)] = values
+        u[p, place(z) + 1, c, of_line(q)] = values
         lon_out[p, 0, c, q * height + z] = values[0]
         lon_out[p, 1, c, q * height + z] = values[wide - 1]
 
     def stepped(p, c, q, z):
         i, side = q // 2, q % 2
-        middle = u[p, z + 1, c, of_line(q)]
+        own = place(z) + 1
+        middle = u[p, own, c, of_line(q)]
         if i == 0:
-            before = u[p, z + 1, jnp.maximum(c - 1, 0), of_line(lines - 2 + side)]
-            outside = jnp.where(c == 0, lat_held[side, z], before)
+            before = u[p, own, jnp.maximum(c - 1, 0), of_line(lines - 2 + side)]
+            outside = jnp.where(c == 0, lat_held[side, place(z)], before)
         else:
-            outside = u[p, z + 1, c, of_line(q - 2)]
+            outside = u[p, own, c, of_line(q - 2)]
         if i == DEPTH - 1:
             end = c == chunks - 1
             at = jnp.where(end, (lines - 1 - side) * wide, side * wide)
             inside = u[
-                p, z + 1, jnp.minimum(c + 1, chunks - 1), pl.ds(pl.multiple_of(at, wide), wide)
+                p, own, jnp.minimum(c + 1, chunks - 1), pl.ds(pl.multiple_of(at, wide), wide)
             ]
         else:
-            inside = u[p, z + 1, c, of_line(q + 2)]
-        low, high = u[p, z, c, of_line(q)], u[p, z + 2, c, of_line(q)]
+            inside = u[p, own, c, of_line(q + 2)]
+        bottom, top = u[p, 1, c, of_line(q)], u[p, height, c, of_line(q)]
         if z == 0:
-            low = swapped(jnp.where(low_lanes, u[p, height, c, of_line(q)], low))
+            low = swapped(jnp.where(low_lanes, top, u[p, 0, c, of_line(q)]))
+        else:
+            low = u[p, place(z - 1) + 1, c, of_line(q)]
         if z == height - 1:
-            high = swapped(jnp.where(low_lanes, high, u[p, 1, c, of_line(q)]))
+            high = swapped(jnp.where(low_lanes, u[p, height + 1, c, of_line(q)], bottom))
+        else:
+            high = u[p, place(z + 1) + 1, c, of_line(q)]
         at = pl.ds(q * height + z, 1)
         west = jnp.where(first_cell, lon_in[p, 1, c, at], pltpu.roll(middle, 1, 0))
         east = jnp.where(last_cell, lon_in[p, 0, c, at], pltpu.roll(middle, wide - 1, 0))
         spread = (outside + inside) + (west + east) + (low + high) - 6.0 * middle
-        return middle + ratio[z, c, of_line(q)] * spread + force[z, c, of_line(q)]
+        return middle + ratio[own - 1, c, of_line(q)] * spread + force[own - 1, c, of_line(q)]
 
     def start_loads(c):
         for f in range(3):
@@ -241,52 +254,81 @@
                 load(f, c, side).start()
 
     barrier = pltpu.get_barrier_semaphore()
-    greeted = [{"lev": partner_lev}]
-    greeted += [t(d) for t in (lat_target, lev_target) for d in (0, 1)]
-    greeted += [stat_target(j) for j in range(lon_size - 1)]
-
-    def pack(f, n, c):
+    second = lev - kind + 1
+    near = [{**lat_target(d), "lev": second} for d in (0, 1)]
+    near += [{"lev": lax.rem(second + move, lev_size)} for move in (2, lev_size - 2)]
+    near += [{**stat_target(j), "lev": second} for j in range(lon_size - 1)]
+    partner = {"lev": partner_lev}
+
+    def signal(sem, other):
+        pl.semaphore_signal(sem, inc=1, device_id=other, device_id_type=MESH)
+
+    def meet_partner():
+        @pl.when(kind == 0)
+        def _():
+            pl.semaphore_wait(barrier, 1)
+            signal(met, partner)
+
+        @pl.when(kind == 1)
+        def _():
+            pl.semaphore_wait(met, 1)
+
+    def meet_all():
+        @pl.when(kind == 1)
+        def _():
+            pl.semaphore_wait(barrier, 1 + 2 * len(near))
+            signal(met, partner)
+
+        @pl.when(kind == 0)
+        def _():
+            pl.semaphore_wait(met, 1)
+
+    def pack(f, q, c):
         slot = lax.rem(c, SLOTS)
-        for q in range(lines):
-            i, side = q // 2, q % 2
-            row = staged(c, f, side) + (i if side == 0 else DEPTH - 1 - i)
+        i, side = q // 2, q % 2
+        row = staged(c, f, side) + (i if side == 0 else DEPTH - 1 - i)
+        for n in range(pairs):
             a, b = butterfly(final[row, cells(2 * n)], final[row, cells(2 * n + 1)])
-            plane(f, 2 * n + kind)[c, of_line(q)] = jnp.where(half == 0, a, b)
+            plane(f, kind * pairs + n)[c, of_line(q)] = jnp.where(half == 0, a, b)
             packed[slot, f, n, of_line(q)] = jnp.where(half == 0, b, a)
 
     def pack_all(c, meet=False):
         for f in range(3):
             for side in (0, 1):
                 load(f, c, side).wait()
-            for n in range(pairs):
-                pack(f, n, c)
-                if meet and f == 0 and n == 0:
-                    pl.semaphore_wait(barrier, len(greeted))
-                swap_copy(f, n, c).start()
+                for i in range(DEPTH):
+                    q = 2 * i + side
+                    pack(f, q, c)
+                    if meet and f == 0:
+                        if q == 0:
+                            meet_partner()
+                        swap_copy(f, c, of_line(q)).start()
+            if not (meet and f == 0):
+                swap_copy(f, c).start()
 
     start_loads(0)
-    for other in greeted:
-        pl.semaphore_signal(barrier, inc=1, device_id=other, device_id_type=MESH)
+    for other in [partner, *near]:
+        signal(barrier, other)
     start_loads(1)
     pack_all(0, meet=True)
     start_loads(2)
     pack_all(1)
     start_loads(3)
+    meet_all()
 
     def arrange(c):
         for f in range(3):
-            for n in range(pairs):
-                swap_copy(f, n, c).wait_recv()
+            swap_copy(f, c).wait_recv()
             for q in range(lines):
                 for n in range(pairs):
                     at = of_line(q)
-                    a, b = butterfly(plane(f, 2 * n)[c, at], plane(f, 2 * n + 1)[c, at])
+                    a, b = butterfly(plane(f, n)[c, at], plane(f, pairs + n)[c, at])
                     if f == 0:
                         put(0, c, q, 2 * n, a)
                         put(0, c, q, 2 * n + 1, b)
                     else:
-                        plane(f, 2 * n)[c, at] = a
-                        plane(f, 2 * n + 1)[c, at] = b
+                        plane(f, n)[c, at] = a
+                        plane(f, pairs + n)[c, at] = b
             if f == 0:
                 send_faces(0, c)
 
@@ -307,13 +349,12 @@
             else:
                 for n in range(pairs):
                     a, b = butterfly(stepped(p, c, q, 2 * n), stepped(p, c, q, 2 * n + 1))
-                    ratio[2 * n, c, of_line(q)] = a
-                    ratio[2 * n + 1, c, of_line(q)] = b
+                    ratio[n, c, of_line(q)] = a
+                    ratio[pairs + n, c, of_line(q)] = b
         if s < STEPS:
             send_faces(q_, c)
         else:
-            for n in range(pairs):
-                back_copy(n, c).start()
+            back_copy(c).start()
 
     def wave(k, carry):
         @pl.when(k < chunks)
@@ -324,8 +365,7 @@
         def _():
             c = k + SLOTS
             for f in range(3):
-                for n in range(pairs):
-                    swap_copy(f, n, c - SLOTS).wait_send()
+                swap_copy(f, c - SLOTS).wait_send()
             pack_all(c)
 
             @pl.when(c + 2 < chunks)
@@ -370,13 +410,12 @@
         stat_copy(j, end).start()
 
     def whole(c, q, n):
-        own = ratio[2 * n + kind, c, of_line(q)]
+        own = ratio[kind * pairs + n, c, of_line(q)]
         other = score[c * pairs + n, of_line(q)]
         return butterfly(jnp.where(half == 0, own, other), jnp.where(half == 0, other, own))
 
     def restore(c):
-        for n in range(pairs):
-            back_copy(n, c).wait_recv()
+        back_copy(c).wait_recv()
         for q in range(lines):
             row = row_of(c, q // 2, q % 2)
             for n in range(pairs):
@@ -427,8 +466,8 @@
             jnp.where(first, pltpu.roll(a, members // 2, 1), b),
         )
 
+    back_copy(end).wait_recv()
     for n in range(pairs):
-        back_copy(n, end).wait_recv()
         for q in range(lines):
             row = row_of(end, q // 2, q % 2)
             for z, values in zip((2 * n, 2 * n + 1), whole(end, q, n)):
@@ -436,7 +475,7 @@
     for n in range(pairs):
         for q in range(lines):
             row = row_of(end, q // 2, q % 2)
-            ours = 2 * n + kind
+            ours = kind * pairs + n
             means, scales = (
                 spread_out(moment_out[q, pl.ds(o + ours, 1)], moment_in[q, pl.ds(o + ours, 1)])
                 for o in (0, height)
@@ -446,8 +485,7 @@
 
     def settle(c, carry):
         wait_sent((STEPS - 1) % 2, c)
-        for n in range(pairs):
-            back_copy(n, c).wait_send()
+        back_copy(c).wait_send()
         for j in range(lon_size - 1):
             stat_copy(j, c).wait_send()
         return carry
@@ -456,8 +494,7 @@
     moment_copy.wait_send()
     for c in range(chunks - SLOTS, chunks):
         for f in range(3):
-            for n in range(pairs):
-                swap_copy(f, n, c).wait_send()
+            swap_copy(f, c).wait_send()
 
 
 def write_out(score, final, score_hbm, final_hbm, sem):
@@ -502,10 +539,10 @@
             pltpu.VMEM((2 * DEPTH, 2 * height, members), f32),
             pltpu.VMEM((2 * DEPTH, 2 * height, members), f32),
             dma((3, 2, 2)),
-            dma((SLOTS, 3, pairs)),
-            dma((chunks, 3, pairs)),
-            dma((chunks, pairs)),
-            dma((chunks, pairs)),
+            dma((SLOTS, 3)),
+            dma((chunks, 3)),
+            dma((chunks,)),
+            dma((chunks,)),
             dma((2, 2, chunks)),
             dma((2, 2, chunks)),
             dma((2, 2, chunks)),
@@ -516,6 +553,7 @@
             dma((others, chunks)),
             dma,
             dma,
+            pltpu.SemaphoreType.REGULAR,
         ],
         compiler_params=pltpu.CompilerParams(
             collective_id=0, has_side_effects=True, vmem_limit_bytes=int(47.25 * 2**20)

time: 376 us -> 373 us (level)
  no operation moved by 1% of the time
where the time goes in v4:
time: 373 us
  Pallas kernels  373 us (100%)
    pallas_call x1, Pallas kernels, local(): pl.pallas_call(functools.partial(kernel, sizes), out_shape=(pltpu.VMEM(fl...  367 us

profile of v4, /device:TPU:0, one launch (start us, length us, event | category | flops | bytes accessed | tf_op | source)
XLA Modules:
  0.0 373.2 jit_solution(1730650255237587568)
XLA Ops:
  0.6 366.6 %shard_map.50 = (f32[32,512,128]{2,1,0:T(8,128)S(1)}, f32[32,512,128]{2,1,0:T(8,128)S(1)}) custom-call(f32[32,512,128]{2,1,0:T(8,128)} %bitcast.5, f32[32,512,128]{2,1,0:T(8,128)} %bitcast.6, f32[32,512,128]{2,1,0:T(8,128)} %bitcast.7), custom_call_target="tpu_custom_call" | custom-call | tf_op jit(solution)/shard_map/pallas_call | solution.py:523
  367.2 6.0 %shard_map.51 = (f32[32,512,128]{2,1,0:T(8,128)}, f32[32,512,128]{2,1,0:T(8,128)}) custom-call(f32[32,512,128]{2,1,0:T(8,128)S(1)} %get-tuple-element.6.score, f32[32,512,128]{2,1,0:T(8,128)S(1)} %get-tuple-element.7.final), custom_call_target="tpu_custom_call" | custom-call | tf_op jit(solution)/shard_map/pallas_call | solution.py:562

commit v5 on v4

--- a/solution.py
+++ b/solution.py
@@ -134,14 +134,17 @@
             {"lev": partner_lev},
         )
 
-    def back_copy(c):
+    def back_copy(c, q=None):
+        at = pl.ds(0, slab) if q is None else pl.ds(q * wide, wide)
         return remote(
-            ratio.at[pl.ds((1 - kind) * pairs, pairs), c],
-            score.at[pl.ds(c * pairs, pairs)],
+            ratio.at[pl.ds((1 - kind) * pairs, pairs), c, at],
+            score.at[pl.ds(c * pairs, pairs), at],
             back_send.at[c],
-            back_recv.at[c],
+            back_recv.at[c if q is None else chunks + q],
             {"lev": partner_lev},
         )
+
+    last_lines = [q for side in (1, 0) for q in range(side, lines, 2)]
 
     def lev_copy(p, d, c):
         src, dst = ((1, height + 1), (height, 0))[d]
@@ -354,7 +357,15 @@
         if s < STEPS:
             send_faces(q_, c)
         else:
-            back_copy(c).start()
+
+            @pl.when(c < chunks - 1)
+            def _():
+                back_copy(c).start()
+
+            @pl.when(c == chunks - 1)
+            def _():
+                for q in last_lines:
+                    back_copy(chunks - 1, q).start()
 
     def wave(k, carry):
         @pl.when(k < chunks)
@@ -466,15 +477,16 @@
             jnp.where(first, pltpu.roll(a, members // 2, 1), b),
         )
 
-    back_copy(end).wait_recv()
-    for n in range(pairs):
-        for q in range(lines):
-            row = row_of(end, q // 2, q % 2)
+    def bring(q):
+        back_copy(end, q).wait_recv()
+        row = row_of(end, q // 2, q % 2)
+        for n in range(pairs):
             for z, values in zip((2 * n, 2 * n + 1), whole(end, q, n)):
                 final[row, cells(z)] = values
-    for n in range(pairs):
-        for q in range(lines):
-            row = row_of(end, q // 2, q % 2)
+
+    def rate(q):
+        row = row_of(end, q // 2, q % 2)
+        for n in range(pairs):
             ours = kind * pairs + n
             means, scales = (
                 spread_out(moment_out[q, pl.ds(o + ours, 1)], moment_in[q, pl.ds(o + ours, 1)])
@@ -482,6 +494,14 @@
             )
             for z, m, k in zip((2 * n, 2 * n + 1), means, scales):
                 score[row, cells(z)] = (final[row, cells(z)] - m) * k
+
+    for q in last_lines[:DEPTH]:
+        bring(q)
+        rate(q)
+    for q in last_lines[DEPTH:]:
+        bring(q)
+    for q in last_lines[DEPTH:]:
+        rate(q)
 
     def settle(c, carry):
         wait_sent((STEPS - 1) % 2, c)
@@ -542,7 +562,7 @@
             dma((SLOTS, 3)),
             dma((chunks, 3)),
             dma((chunks,)),
-            dma((chunks,)),
+            dma((chunks + 2 * DEPTH,)),
             dma((2, 2, chunks)),
             dma((2, 2, chunks)),
             dma((2, 2, chunks)),

time: 373 us -> 374 us (level)
  no operation moved by 1% of the time
where the time goes in v5:
time: 374 us; the launch traced here: 373 us
  Pallas kernels  373 us (100%)
    pallas_call x1, Pallas kernels, local(): pl.pallas_call(functools.partial(kernel, sizes), out_shape=(pltpu.VMEM(fl...  367 us

profile of v5, /device:TPU:0, one launch (start us, length us, event | category | flops | bytes accessed | tf_op | source)
XLA Modules:
  0.0 373.4 jit_solution(10257480365373685341)
XLA Ops:
  0.6 366.8 %shard_map.50 = (f32[32,512,128]{2,1,0:T(8,128)S(1)}, f32[32,512,128]{2,1,0:T(8,128)S(1)}) custom-call(f32[32,512,128]{2,1,0:T(8,128)} %bitcast.5, f32[32,512,128]{2,1,0:T(8,128)} %bitcast.6, f32[32,512,128]{2,1,0:T(8,128)} %bitcast.7), custom_call_target="tpu_custom_call" | custom-call | tf_op jit(solution)/shard_map/pallas_call | solution.py:543
  367.5 6.0 %shard_map.51 = (f32[32,512,128]{2,1,0:T(8,128)}, f32[32,512,128]{2,1,0:T(8,128)}) custom-call(f32[32,512,128]{2,1,0:T(8,128)S(1)} %get-tuple-element.6.score, f32[32,512,128]{2,1,0:T(8,128)S(1)} %get-tuple-element.7.final), custom_call_target="tpu_custom_call" | custom-call | tf_op jit(solution)/shard_map/pallas_call | solution.py:582

commit v6 on v4

--- a/solution.py
+++ b/solution.py
@@ -10,7 +10,7 @@
 STEPS = 4
 DEPTH = 2
 SLOTS = 2
-PARTS = 8
+PARTS = 16
 MESH = pl.DeviceIdType.MESH
 
 

time: 373 us -> 373 us (level)
  no operation moved by 1% of the time
where the time goes in v6:
time: 373 us
  Pallas kernels  373 us (100%)
    pallas_call x1, Pallas kernels, local(): pl.pallas_call(functools.partial(kernel, sizes), out_shape=(pltpu.VMEM(fl...  367 us

profile of v6, /device:TPU:0, one launch (start us, length us, event | category | flops | bytes accessed | tf_op | source)
XLA Modules:
  0.0 373.3 jit_solution(12078383467988285001)
XLA Ops:
  0.6 366.6 %shard_map.50 = (f32[32,512,128]{2,1,0:T(8,128)S(1)}, f32[32,512,128]{2,1,0:T(8,128)S(1)}) custom-call(f32[32,512,128]{2,1,0:T(8,128)} %bitcast.5, f32[32,512,128]{2,1,0:T(8,128)} %bitcast.6, f32[32,512,128]{2,1,0:T(8,128)} %bitcast.7), custom_call_target="tpu_custom_call" | custom-call | tf_op jit(solution)/shard_map/pallas_call | solution.py:523
  367.2 6.1 %shard_map.51 = (f32[32,512,128]{2,1,0:T(8,128)}, f32[32,512,128]{2,1,0:T(8,128)}) custom-call(f32[32,512,128]{2,1,0:T(8,128)S(1)} %get-tuple-element.6.score, f32[32,512,128]{2,1,0:T(8,128)S(1)} %get-tuple-element.7.final), custom_call_target="tpu_custom_call" | custom-call | tf_op jit(solution)/shard_map/pallas_call | solution.py:562
